TPU v7x, 32 devices: a whole 2x2x4 slice. The times are simulated.
32 devices in a mesh: row: 8 (over y, x, core), col: 4 (over z).
Axes of the slice: x: 2, y: 2, z: 4, core: 2. Of those that a mesh axis runs over, the one named last changes fastest.
Arguments:
- state: float32 [2048, 4, 1024], P('row', 'col'), may hold values from -6 to 6
- coupling: bfloat16 [2048, 4, 1024], P('row', 'col'), may hold values from -2 to 2, as said below
- coupling_t: bfloat16 [2, 2048, 4, 1024], P(None, 'row', 'col'), may hold values from -2 to 2, as said below
- factor: float32 [4, 4, 256, 256], P(None, 'col', 'row'), may hold values from -0.3 to 1.3
- cofactor: float32 [4, 4, 256, 256], P(None, 'col', 'row'), may hold values from -0.3 to 1.3
- rates: float32 [4, 4, 256], P(None, 'col'), may hold values from 0.5 to 2
Outputs:
- updated_state: float32 [2048, 4, 1024], P('row', 'col')
Inputs may be any that keep to these rules, and one draw needn't show every extreme that they name: coupling and coupling_t hold the same matrix A; its blocks A(i, k) are zero unless k > i. coupling_t holds the transposed blocks of the A in coupling.
All inputs are finite; a program needn't handle non-finite values.
Results may differ from a plain program's by a relative error of at most 0.0003.
Values may be sent and summed in bfloat16 or wider, within the bound.
A program may use at most 64 MiB of HBM per device.

v0:
```python
import jax
import jax.numpy as jnp
from jax import lax
from jax.sharding import PartitionSpec as P

STEPS = 2


HIGHEST_PRECISION = lax.Precision.HIGHEST


def broadcast(block, axis, source):
    block = jnp.where(lax.axis_index(axis) == source, block, jnp.zeros_like(block))
    return lax.psum(block, axis)


def from_behind(block, axis, distance):
    devices = range(lax.axis_size(axis))
    route = [((i - distance) % len(devices), i) for i in devices]
    return lax.ppermute(block, axis, route)


def solve_block(residual, left_p, left_q, left_e, right_p, right_q, right_e):
    middle = jnp.dot(
        left_q, residual, precision=HIGHEST_PRECISION, preferred_element_type=jnp.float32
    )
    middle = jnp.dot(
        middle, right_q.T, precision=HIGHEST_PRECISION, preferred_element_type=jnp.float32
    )
    middle = middle / (left_e[:, None] + right_e[None, :])
    product = jnp.dot(
        left_p, middle, precision=HIGHEST_PRECISION, preferred_element_type=jnp.float32
    )
    return -jnp.dot(
        product, right_p.T, precision=HIGHEST_PRECISION, preferred_element_type=jnp.float32
    )


def pick_slot(stacked, slot_index):
    return lax.dynamic_index_in_dim(stacked, slot_index, 0, keepdims=False)


def on_device(state, coupling, coupling_t, factor, cofactor, rates):
    row_count = lax.axis_size("row")
    col_count = lax.axis_size("col")
    half_rows = row_count // 2
    order_blocks = 2 * row_count
    col_slots = order_blocks // col_count
    block_size = state.shape[0]
    row_index = lax.axis_index("row")
    col_index = lax.axis_index("col")
    blocks = jnp.transpose(state.reshape(block_size, col_slots, block_size), (1, 0, 2))
    full_p, full_q = (
        lax.all_gather(factor, "row", axis=2, tiled=True),
        lax.all_gather(cofactor, "row", axis=2, tiled=True),
    )
    right_ps = full_p.reshape(col_slots, block_size, block_size)
    right_qs = full_q.reshape(col_slots, block_size, block_size)
    right_es = rates.reshape(col_slots, block_size)
    own_slot = row_index // col_count
    picked = (
        pick_slot(right_ps, own_slot),
        pick_slot(right_qs, own_slot),
        pick_slot(right_es, own_slot),
    )
    left_p, left_q, left_e = (
        broadcast(picked[0], "col", row_index % col_count),
        broadcast(picked[1], "col", row_index % col_count),
        broadcast(picked[2], "col", row_index % col_count),
    )
    upper_row = coupling.reshape(block_size, col_slots * block_size)
    lower_pair = coupling_t.reshape(2, block_size, col_slots * block_size)
    my_columns = col_index + col_count * jnp.arange(col_slots, dtype=jnp.int32)
    upper_now = upper_row
    for wave_step in range(STEPS):
        antidiag = order_blocks - 1 - wave_step
        partner = antidiag - row_index
        owner_col = partner % col_count
        slot_here = partner // col_count
        usable = row_index <= partner
        residual = pick_slot(blocks, slot_here)
        solution = solve_block(
            residual,
            left_p,
            left_q,
            left_e,
            pick_slot(right_ps, slot_here),
            pick_slot(right_qs, slot_here),
            pick_slot(right_es, slot_here),
        )
        solution = jnp.where(usable, solution, 0.0)
        written = jnp.where(usable & (col_index == owner_col), solution, residual)
        blocks = lax.dynamic_update_index_in_dim(blocks, written, slot_here, 0)
        shared = broadcast(solution, "col", owner_col)
        mirror = antidiag - my_columns
        use_row = mirror <= my_columns
        sources = jnp.clip(jnp.where(use_row, mirror, my_columns), 0, row_count - 1)
        offered = jnp.where((sources == row_index)[:, None, None], shared[None], 0.0)
        fetched = lax.psum(offered, "row")
        partner_blocks = jnp.where(use_row[:, None, None], fetched, jnp.swapaxes(fetched, 1, 2))
        if wave_step > 0:
            upper_now = from_behind(upper_row, "col", (col_count - wave_step) % col_count)
        receiver = (row_index - wave_step - half_rows) % row_count
        send_slot = jnp.where(receiver + wave_step >= row_count, 1, 0)
        send_piece = pick_slot(lower_pair, send_slot)
        lower_now = from_behind(send_piece, "row", (half_rows - wave_step) % row_count)
        upper_view = upper_now.reshape(block_size, col_slots, block_size)
        rolled = jnp.where(
            (col_index + wave_step) // col_count == 1, jnp.roll(upper_view, -1, axis=1), upper_view
        )
        lower_view = lower_now.reshape(block_size, col_slots, block_size)
        left_terms = jnp.einsum(
            "aub,ubc->uac", rolled.astype(jnp.float32), partner_blocks, precision=HIGHEST_PRECISION
        )
        right_terms = jnp.einsum(
            "ab,buc->uac", shared, lower_view.astype(jnp.float32), precision=HIGHEST_PRECISION
        )
        targets = (row_index <= my_columns) & (row_index + my_columns < antidiag)
        blocks = blocks - jnp.where(targets[:, None, None], left_terms + right_terms, 0.0)
    return jnp.transpose(blocks, (1, 0, 2)).reshape(block_size, 1, col_slots * block_size)


def solution(mesh):
    return jax.shard_map(
        on_device,
        mesh=mesh,
        in_specs=(
            P("row", "col", None),
            P("row", "col", None),
            P(None, "row", "col", None),
            P(None, "col", "row", None),
            P(None, "col", "row", None),
            P(None, "col", None),
        ),
        out_specs=P("row", "col", None),
        check_vma=False,
    )
```

profile of v0, /device:TPU:16, one launch (start us, length us, event | category | flops | bytes accessed | tf_op | source)
XLA Modules:
  0.0 326.9 jit_solution(1007737203448546680)
XLA Ops:
  6.5 0.7 all-gather.3.cloned.1.call-update
  7.3 0.0 all-gather.5.cloned.1.call-start
  7.3 0.7 all-gather.5.cloned.1.call-update
  8.0 0.0 all-reduce.15.cloned.1.call-start
  8.1 25.6 %all-gather.3.cloned.1.call-done = f32[4,1,256,256]{3,2,1,0:T(8,128)} async-done(((f32[4,1,32,256]{3,2,1,0:T(8,128)}), f32[4,1,256,256]{3,2,1,0:T(8,128)}) %all-gather.3.cloned.1.call-update) | async-done | bytes 1048592 | tf_op jit(solution)/shard_map/all_gather | solution.py:54
  33.7 1.7 select_bitcast_fusion.1
  35.4 23.6 %all-gather.5.cloned.1.call-done = f32[4,1,256,256]{3,2,1,0:T(8,128)} async-done(((f32[4,1,32,256]{3,2,1,0:T(8,128)}), f32[4,1,256,256]{3,2,1,0:T(8,128)}) %all-gather.5.cloned.1.call-update) | async-done | bytes 1048592 | tf_op jit(solution)/shard_map/all_gather | solution.py:55
  59.0 1.7 select_bitcast_fusion
  60.7 0.0 all-reduce.15.cloned.1.call-update
  60.7 0.0 all-reduce.7.cloned.1.call-start
  60.8 1.0 copy.19
  61.7 0.1 copy.51
  61.8 0.0 copy-start.15
  61.9 0.7 copy-done.15
  62.5 9.0 %psum.51 = f32[256]{0:T(256)S(1)} all-reduce(f32[256]{0:T(256)S(1)} %bitcast.106), channel_id=1, replica_groups=mesh['row'=8,'col'=4] {'col'}, use_global_device_ids=true, to_apply=%region_2.3 | all-reduce | flops 256 | bytes 2048 | tf_op jit(solution)/shard_map/psum | solution.py:14
  71.6 28.2 %all-reduce.15.cloned.1.call-done = (f32[256,256]{1,0:T(8,128)}, f32[256,256]{1,0:T(8,128)}) async-done(((f32[256,256]{1,0:T(8,128)}, f32[256,256]{1,0:T(8,128)}), (f32[256,256]{1,0:T(8,128)}, f32[256,256]{1,0:T(8,128)})) %all-reduce.15.cloned.1.call-update) | async-done | bytes 524304 | tf_op jit(solution)/shard_map/psum | solution.py:14
  99.7 1.4 fusion.24
  101.1 1.4 convolution_divide_fusion.1
  102.5 0.4 fusion.45
  102.9 0.0 copy-start.10
  102.9 1.5 bitcast_dynamic-update-slice_fusion.1
  104.4 0.0 copy-start.2
  104.4 0.8 broadcast_select_fusion.3
  105.2 0.0 all-reduce.7.cloned.1.call-update
  105.2 0.0 all-reduce.9.cloned.1.call-start
  105.3 1.1 dynamic-slice_bitcast_fusion
  106.4 1.5 collective-permute-start
  107.9 33.0 %all-reduce.7.cloned.1.call-done = f32[256,256]{0,1:T(8,128)} async-done(((f32[256,256]{0,1:T(8,128)}), f32[256,256]{0,1:T(8,128)}) %all-reduce.7.cloned.1.call-update) | async-done | bytes 262160 | tf_op jit(solution)/shard_map/psum | solution.py:14
  140.9 2.1 broadcast_select_fusion.1
  143.0 0.0 all-reduce.9.cloned.1.call-update
  143.0 0.0 all-reduce.11.cloned.1.call-start
  143.1 1.0 copy-done.12
  144.0 0.4 reshape_reshape.3
  144.4 0.2 slice.19
  144.6 0.3 slice.18
  144.9 0.7 copy.46
  145.6 0.1 copy.47
  145.7 0.2 copy.24
  145.9 54.9 %all-reduce.9.cloned.1.call-done = f32[4,256,256]{1,2,0:T(8,128)} async-done(((f32[4,256,256]{1,2,0:T(8,128)}), f32[4,256,256]{1,2,0:T(8,128)}) %all-reduce.9.cloned.1.call-update) | async-done | bytes 1048592 | tf_op jit(solution)/shard_map/psum | solution.py:99
  200.8 1.6 copy.23
  202.5 1.7 fusion.7
  204.3 0.6 fusion.4
  205.0 0.9 copy-done.11
  205.9 0.4 fusion.19
  206.3 1.4 convolution_divide_fusion
  207.7 0.4 fusion.46
  208.1 1.4 bitcast_dynamic-update-slice_fusion
  209.6 0.7 broadcast_select_fusion.2
  210.3 0.0 all-reduce.11.cloned.1.call-update
  210.3 0.0 all-reduce.13.cloned.1.call-start
  210.4 0.1 collective-permute-start.2
  210.4 0.3 copy-done.13
  210.7 0.5 collective-permute-start.1
  211.3 39.3 %all-reduce.11.cloned.1.call-done = f32[256,256]{0,1:T(8,128)} async-done(((f32[256,256]{0,1:T(8,128)}), f32[256,256]{0,1:T(8,128)}) %all-reduce.11.cloned.1.call-update) | async-done | bytes 262160 | tf_op jit(solution)/shard_map/psum | solution.py:14
  250.6 2.1 broadcast_select_fusion
  252.7 0.0 all-reduce.13.cloned.1.call-update
  252.8 0.8 copy-done.4
  253.5 0.6 slice.21
  254.2 1.3 copy.30
  255.5 0.6 convolution_bitcast_fusion
  256.1 54.5 %all-reduce.13.cloned.1.call-done = f32[4,256,256]{1,2,0:T(8,128)} async-done(((f32[4,256,256]{1,2,0:T(8,128)}), f32[4,256,256]{1,2,0:T(8,128)}) %all-reduce.13.cloned.1.call-update) | async-done | bytes 1048592 | tf_op jit(solution)/shard_map/psum | solution.py:99
  310.6 2.6 copy.29
  313.3 3.2 fusion.1
  316.4 3.6 %copy.32 = f32[256,1,1024]{2,1,0:T(1,128)} copy(f32[256,1,1024]{0,2,1:T(8,128)} %bitcast.98) | data formatting | bytes 2097152 | tf_op jit(solution)/shard_map/reshape | solution.py:120
  (37 shorter events, 0.2 us)
Async XLA Ops:
  6.5 54.2 %copy-start.9 = (f32[256,1,1024]{2,1,0:T(1,128)S(1)}, f32[256,1,1024]{2,1,0:T(1,128)}, u32[]{:S(2)}) copy-start(f32[256,1,1024]{2,1,0:T(1,128)} %param.6) | copy-start | bytes 3145732
  6.5 27.2 %all-gather.3.cloned.1.call-start = ((), (), s32[]{:S(2)}) async-start(), calls=%async_computation | async-start | bytes 1179648 | tf_op jit(solution)/shard_map/all_gather | solution.py:54
  7.3 51.8 %all-gather.5.cloned.1.call-start = ((), (), s32[]{:S(2)}) async-start(), calls=%async_computation.1 | async-start | bytes 1179648 | tf_op jit(solution)/shard_map/all_gather | solution.py:55
  8.0 91.7 %all-reduce.15.cloned.1.call-start = ((), (), s32[]{:S(2)}) async-start(), calls=%async_computation.6 | async-start | bytes 1048576 | tf_op jit(solution)/shard_map/psum | solution.py:14
  60.7 80.2 %all-reduce.7.cloned.1.call-start = ((), (), s32[]{:S(2)}) async-start(), calls=%async_computation.2 | async-start | bytes 524288 | tf_op jit(solution)/shard_map/psum | solution.py:14
  61.8 0.7 copy-start.15
  101.1 1.4 copy-start.5
  102.9 2.4 copy-start.10
  104.4 2.0 copy-start.2
  105.2 95.6 %all-reduce.9.cloned.1.call-start = ((), (), s32[]{:S(2)}) async-start(), calls=%async_computation.3 | async-start | bytes 2097152 | tf_op jit(solution)/shard_map/psum | solution.py:99
  106.4 39.3 %collective-permute-start = (bf16[256,1024]{1,0:T(8,128)(2,1)}, bf16[256,1024]{1,0:T(8,128)(2,1)S(1)}, u32[]{:S(2)}, u32[]{:S(2)}) collective-permute-start(bf16[256,1024]{1,0:T(8,128)(2,1)} %get-tuple-element.8), channel_id=1, source_target_pairs={{16,0},{20,4},{24,8},{28,12},{0,16},{4,20},{8,24},{12,28},{17,1},{... | collective-permute-start | bytes 1572872 | tf_op jit(solution)/shard_map/ppermute | solution.py:20
  143.0 1.0 copy-start.12
  143.0 107.6 %all-reduce.11.cloned.1.call-start = ((), (), s32[]{:S(2)}) async-start(), calls=%async_computation.4 | async-start | bytes 524288 | tf_op jit(solution)/shard_map/psum | solution.py:14
  200.8 1.7 copy-start
  202.5 1.8 copy-start.3
  202.5 1.8 copy-start.7
  204.9 1.0 copy-start.11
  206.3 1.4 copy-start.6
  208.1 2.3 copy-start.14
  209.6 1.1 copy-start.13
  210.3 100.3 %all-reduce.13.cloned.1.call-start = ((), (), s32[]{:S(2)}) async-start(), calls=%async_computation.5 | async-start | bytes 2097152 | tf_op jit(solution)/shard_map/psum | solution.py:99
  210.4 43.8 %collective-permute-start.2 = (bf16[256,1024]{1,0:T(8,128)(2,1)S(1)}, bf16[256,1024]{1,0:T(8,128)(2,1)}, u32[]{:S(2)}, u32[]{:S(2)}) collective-permute-start(bf16[256,1024]{1,0:T(8,128)(2,1)S(1)} %copy-done.14), channel_id=1, source_target_pairs={{20,0},{24,4},{28,8},{0,12},{4,16},{8,20},{12,24},{16,28},{21,1},{... | collective-permute-start | bytes 1572872 | tf_op jit(solution)/shard_map/ppermute | solution.py:20
  210.7 42.0 %collective-permute-start.1 = (bf16[256,1024]{1,0:T(8,128)(2,1)S(1)}, bf16[256,1024]{1,0:T(8,128)(2,1)S(1)}, u32[]{:S(2)}, u32[]{:S(2)}) collective-permute-start(bf16[256,1024]{1,0:T(8,128)(2,1)S(1)} %bitcast.105), channel_id=1, source_target_pairs={{1,0},{2,1},{3,2},{0,3},{5,4},{6,5},{7,6},{4,7},{9,8},{10,9},{11,1... | collective-permute-start | bytes 1572872 | tf_op jit(solution)/shard_map/ppermute | solution.py:20
  252.7 0.8 copy-start.4
  254.2 1.3 copy-start.8
  310.6 2.6 copy-start.1
Sparse Core Ops, SparseCore 0:
  9.2 24.4 all-gather.2
  35.6 23.3 all-gather.4
  61.4 38.2 all-reduce.14
  105.3 35.5 all-reduce.6
  143.9 56.8 all-reduce.8
  210.4 40.1 all-reduce.10
  253.8 56.8 all-reduce.12
where the time goes:
time: 329 us; the launch traced here: 327 us
  waiting for transfers between devices  261 us (79%)
  local copies, waits for them, and re-layouts  17.3 us (5%)
  matrix products  14.4 us (4%)
  between operations  14 us (4%)
  blocking collectives  9.05 us (3%)
  other arithmetic  9.03 us (3%)
    psum x2, waiting for transfers between devices, on_device(): fetched = lax.psum(offered, 'row')  109 us
    psum x3, waiting for transfers between devices, broadcast(): return lax.psum(block, axis)  101 us
    all_gather x1, waiting for transfers between devices, on_device(): lax.all_gather(factor, 'row', axis=2, tiled=True)  25.6 us
    all_gather x1, waiting for transfers between devices, on_device(): lax.all_gather(cofactor, 'row', axis=2, tiled=True)  23.6 us
    psum x1, blocking collectives, broadcast(): return lax.psum(block, axis)  9.05 us
  transfers between devices with their start and end apart: 10, of which 7 were waited for; matrix products, arithmetic and copies ran while one was open for 4% of the time, Pallas kernels for 0%

commit v1 on v0

v1 whole, which is shorter than its diff:
```python
import functools

import jax
import jax.numpy as jnp
from jax import lax
from jax.experimental import pallas as pl
from jax.experimental.pallas import tpu as pltpu
from jax.sharding import PartitionSpec as P

STEPS = 2
MESH = pl.DeviceIdType.MESH
F32 = jnp.float32
NN = (((1,), (0,)), ((), ()))
NT = (((1,), (1,)), ((), ()))


def halves(x):
    hi = x.astype(jnp.bfloat16)
    return hi, (x - hi.astype(F32)).astype(jnp.bfloat16)


def mm(a, b, dims):
    return lax.dot_general(a, b, dims, preferred_element_type=F32)


def dot3(a, b, dims):
    ah, al = halves(a)
    bh, bl = halves(b)
    return mm(ah, bh, dims) + (mm(ah, bl, dims) + mm(al, bh, dims))


def kernel(R, C, U, BS, SR, state, upper, lower, factor, cofactor, rates, out,
           ops, ebuf, xz, atb, an, ops_sem, e_sem, xz_sem, at_sem, an_sem, send_sem):
    H = R // 2
    r = lax.axis_index("row")
    c = lax.axis_index("col")
    d = [2 * R - 1 - s for s in range(STEPS)]

    def owner(row, s):
        return (d[s] - row) % C

    o = [owner(r, s) for s in range(STEPS)]
    sends = []

    def send(cond, src, dst, sem, dev):
        k = len(sends)
        copy = pltpu.make_async_remote_copy(
            src_ref=src, dst_ref=dst, send_sem=send_sem.at[k], recv_sem=sem,
            device_id=dev, device_id_type=MESH)
        sends.append((cond, copy))

        @pl.when(cond)
        def _():
            copy.start()

    def send_or_local(cond, src, dst, sem, dev):
        mine = (dev[0] == r) & (dev[1] == c)
        send(cond & jnp.logical_not(mine), src, dst, sem, dev)

        @pl.when(cond & mine)
        def _():
            pltpu.make_async_copy(src, dst, sem).start()

    def arrive(ref, sem):
        pltpu.make_async_copy(ref, ref, sem).wait()

    def slot(u):
        if isinstance(u, int):
            return pl.ds(u * BS, BS)
        return pl.ds(pl.multiple_of(u * BS, BS), BS)

    def target(row, m, s):
        return (row <= m) & (row + m < d[s])

    rows = pl.ds(pl.multiple_of(r * SR, SR), SR)
    for src, base in ((cofactor, 0), (factor, 2)):
        for s in range(STEPS):
            for u in range(U):
                m = c + C * u
                if u >= U // 2 - s:
                    to = d[s] - m
                    send_or_local((to >= 0) & (to < R), src.at[u], ops.at[base + 1, rows],
                                  ops_sem.at[base + 1], (to, c))
                if u < U // 2:
                    send_or_local(m < R, src.at[u], ops.at[base, rows],
                                  ops_sem.at[base], (m, owner(m, s)))
    for s in range(STEPS):
        send_or_local(c == r % C, rates, ebuf, e_sem.at[0], (r, o[s]))

    def send_lower(s):
        to = (r + R - s - H) % R
        for u in reversed(range(U)):
            m = c + C * u
            send(target(to, m, s) & (to + s < R), lower.at[:, slot(u)], atb.at[s, u],
                 at_sem.at[s, u], (to, c))

    def send_upper():
        for u in range(U):
            m = c + C * u - 1
            to = (c + C - 1) % C
            to_u = jnp.maximum(jnp.where(c >= 1, u, u - 1), 0)
            send((m >= 0) & target(r, m, 1), upper.at[:, slot(u)], an.at[to_u],
                 an_sem.at[to_u], (r, to))

    send_lower(0)
    send_upper()
    out[...] = state[...]

    def spread(s):
        own_col = r % C == c
        k = jnp.where(own_col, r // C, (d[s] - r) // C)
        for back in range(1, R):
            to = jnp.maximum(r - back, 0)
            send((r >= back) & (own_col | (c == o[s])), xz.at[s, U], xz.at[s, k],
                 xz_sem.at[s, k], (to, c))

    def share_row(s):
        for hop in range(1, C):
            to = (c + C - hop) % C
            send(c == o[s], xz.at[s, U], xz.at[s, U], xz_sem.at[s, U], (r, to))

    def solve(s):
        q = (d[s] - r) // C
        arrive(ebuf, e_sem.at[0])
        left_e = jnp.transpose(jnp.broadcast_to(ebuf[pl.ds(r // C, 1), :], (BS, BS)))
        rate = left_e + rates[pl.ds(q, 1), :]
        arrive(ops.at[0], ops_sem.at[0])
        mid = dot3(ops[0], out[:, slot(q)], NN)
        arrive(ops.at[1], ops_sem.at[1])
        mid = dot3(mid, ops[1], NT) / rate
        arrive(ops.at[2], ops_sem.at[2])
        mid = dot3(ops[2], mid, NN)
        arrive(ops.at[3], ops_sem.at[3])
        x = -dot3(mid, ops[3], NT)
        xz[s, U] = x
        out[:, slot(q)] = x

    def z_index(u, s):
        m = c + C * u
        j = jnp.where(d[s] - m <= m, d[s] - m, m)
        k = jnp.where(j == r, U, jnp.where(j % C == c, j // C, u))
        return j, k

    def await_z(u, s):
        j, k = z_index(u, s)
        landed = r < j
        if u >= U // 2:
            landed = landed & (j % C != c)

        @pl.when(landed)
        def _():
            arrive(xz.at[s, u], xz_sem.at[s, u])

    def update(u, s):
        m = c + C * u
        j, k = z_index(u, s)
        arrive(atb.at[s, u], at_sem.at[s, u])
        if s > 0:
            arrive(an.at[u], an_sem.at[u])
            a = an[u]
        else:
            a = upper[:, slot(u)]
        xh, xl = halves(xz[s, U])
        at = atb[s, u]
        out[:, slot(u)] -= mm(xh, at, NN) + mm(xl, at, NN)
        zh, zl = halves(xz[s, k])
        straight = d[s] - m <= m

        @pl.when(straight)
        def _():
            out[:, slot(u)] -= mm(a, zh, NN) + mm(a, zl, NN)

        @pl.when(jnp.logical_not(straight))
        def _():
            out[:, slot(u)] -= mm(a, zh, NT) + mm(a, zl, NT)

    def step_update(u, s):
        await_z(u, s)

        @pl.when(target(r, c + C * u, s))
        def _():
            update(u, s)

    @pl.when(c == o[0])
    def _():
        solve(0)

    @pl.when(c != o[0])
    def _():
        arrive(xz.at[0, U], xz_sem.at[0, U])

    share_row(0)
    spread(0)
    send_lower(1)

    q1 = (d[1] - r) // C
    first = c == o[1]
    for u in range(U // 2 - 1, U):
        @pl.when(first & (q1 == u))
        def _(u=u):
            step_update(u, 0)

    @pl.when(first)
    def _():
        solve(1)

    share_row(1)

    def rest():
        for u in range(U):
            skip = first & (q1 == u)

            @pl.when(jnp.logical_not(skip))
            def _(u=u):
                step_update(u, 0)

    @pl.when(jnp.logical_not(first))
    def _():
        rest()
        arrive(xz.at[1, U], xz_sem.at[1, U])

    spread(1)

    @pl.when(first)
    def _():
        rest()

    for u in range(U):
        step_update(u, 1)

    for cond, copy in sends:
        @pl.when(cond)
        def _(copy=copy):
            copy.wait_send()


def on_device(state, coupling, coupling_t, factor, cofactor, rates):
    R = lax.axis_size("row")
    C = lax.axis_size("col")
    U = 2 * R // C
    BS = state.shape[0]
    SR = factor.shape[2]
    flat = U * BS
    vmem = pl.BlockSpec(memory_space=pltpu.VMEM)
    n_sends = 2 * STEPS * (2 * U) + STEPS + (STEPS + 1) * U + STEPS * (R - 1 + C - 1)
    dma = pltpu.SemaphoreType.DMA
    out = pl.pallas_call(
        functools.partial(kernel, R, C, U, BS, SR),
        out_shape=jax.ShapeDtypeStruct((BS, flat), F32),
        in_specs=[vmem] * 6,
        out_specs=vmem,
        scratch_shapes=[
            pltpu.VMEM((4, BS, BS), F32),
            pltpu.VMEM((U, BS), F32),
            pltpu.VMEM((STEPS, U + 1, BS, BS), F32),
            pltpu.VMEM((STEPS, U, BS, BS), jnp.bfloat16),
            pltpu.VMEM((U, BS, BS), jnp.bfloat16),
            dma((4,)),
            dma((1,)),
            dma((STEPS, U + 1)),
            dma((STEPS, U)),
            dma((U,)),
            dma((n_sends,)),
        ],
        compiler_params=pltpu.CompilerParams(
            has_side_effects=True, vmem_limit_bytes=48 * 1024 * 1024),
    )(
        state.reshape(BS, flat),
        coupling.reshape(BS, flat),
        coupling_t[0].reshape(BS, flat),
        factor.reshape(U, SR, BS),
        cofactor.reshape(U, SR, BS),
        rates.reshape(U, BS),
    )
    return out.reshape(BS, 1, flat)


def solution(mesh):
    return jax.shard_map(
        on_device,
        mesh=mesh,
        in_specs=(
            P("row", "col", None),
            P("row", "col", None),
            P(None, "row", "col", None),
            P(None, "col", "row", None),
            P(None, "col", "row", None),
            P(None, "col", None),
        ),
        out_specs=P("row", "col", None),
        check_vma=False,
    )
```

time: 329 us -> 72.6 us (0.22)
  waiting for transfers between devices: 261 us -> 0 us
  Pallas kernels: 0 us -> 67.5 us
  matrix products: 14.4 us -> 0 us
  between operations: 14 us -> 0.05 us
  local copies, waits for them, and re-layouts: 17.3 us -> 4.89 us
  blocking collectives: 9.05 us -> 0 us
  other arithmetic: 9.03 us -> 0 us
    psum x5 -> x0, waiting for transfers between devices: 210 us -> none  [the longest x2 109 us: on_device(): fetched = lax.psum(offered, 'row')]
    pallas_call x0 -> x1, Pallas kernels: none -> 67.5 us  [on_device(): pl.pallas_call(functools.partial(kernel, R, C, U, BS, SR), out_shape=jax....]
    all_gather x2 -> x0, waiting for transfers between devices: 49.3 us -> none  [the longest x1 25.6 us: on_device(): lax.all_gather(factor, 'row', axis=2, tiled=True)]
    dot_general x12 -> x0, matrix products: 14.4 us -> none  [the longest x2 4.93 us: on_device(): jnp.einsum('aub,ubc->uac', rolled.astype(jnp.float32), partner_blocks, pr...]
    psum x1 -> x0, blocking collectives: 9.05 us -> none  [broadcast(): return lax.psum(block, axis)]
    select_n x6 -> x0, other arithmetic: 8.97 us -> none  [the longest x4 4.85 us: broadcast(): jnp.where(lax.axis_index(axis) == source, block, jnp.zeros_like(block))]
    psum x2 -> x0, local copies, waits for them, and re-layouts: 4.26 us -> none  [on_device(): fetched = lax.psum(offered, 'row')]
    unnamed x36 -> x12, local copies, waits for them, and re-layouts: 5.35 us -> 1.76 us
  transfers between devices with their start and end apart: 10 -> 0, of which waited for: 7 -> 0; matrix products, arithmetic and copies ran while one was open for 4% -> 0% of each run, Pallas kernels for 0% -> 0%
where the time goes in v1:
time: 72.6 us; the launch traced here: 72.5 us
  Pallas kernels  67.5 us (93%)
  local copies, waits for them, and re-layouts  4.89 us (7%)
    pallas_call x1, Pallas kernels, on_device(): pl.pallas_call(functools.partial(kernel, R, C, U, BS, SR), out_shape=jax....  67.5 us
    reshape x1, local copies, waits for them, and re-layouts, on_device(): return out.reshape(BS, 1, flat)  2.05 us
    unnamed x12, local copies, waits for them, and re-layouts  1.76 us

profile of v1, /device:TPU:16, one launch (start us, length us, event | category | flops | bytes accessed | tf_op | source)
XLA Modules:
  0.0 72.5 jit_solution(2481524598283146982)
XLA Ops:
  0.0 0.0 copy-start.4
  0.0 0.0 copy-start.3
  0.0 0.7 copy-done.4
  0.7 1.1 %slice_bitcast_fusion.lower = bf16[256,1024]{1,0:T(8,128)(2,1)S(1)} fusion(bf16[2,256,1,1024]{3,1,2,0:T(8,128)(2,1)} %param.8), kind=kLoop, calls=%fused_computation.1 | loop fusion | bytes 1048576 | tf_op jit(solution)/shard_map/reshape;squeeze | solution.py:270
  1.8 0.0 copy-done.3
  1.8 0.0 copy-start
  1.8 0.0 copy-start.1
  1.8 0.0 copy-start.2
  1.8 0.2 copy.12
  2.0 0.8 %copy-done = bf16[256,1,1024]{2,0,1:T(8,128)(2,1)S(1)} copy-done((bf16[256,1,1024]{2,0,1:T(8,128)(2,1)S(1)}, bf16[256,1,1024]{2,0,1:T(8,128)(2,1)}, u32[]{:S(2)}) %copy-start) | copy-done | bytes 524312
  2.8 0.0 copy-done.1
  2.8 0.0 copy-done.2
  2.9 67.5 %shard_map.64 = f32[256,1024]{1,0:T(8,128)S(1)} custom-call(f32[256,1024]{1,0:T(8,128)S(1)} %bitcast.13, bf16[256,1024]{1,0:T(8,128)(2,1)S(1)} %bitcast.14, bf16[256,1024]{1,0:T(8,128)(2,1)S(1)} %slice_bitcast_fusion.lower, f32[4,32,256]{2,1,0:T(8,128)S(1)} %bitcast.15, f32[4,32,256]{2,1,0:T(8,128)S(1)} %bitcast.16, f32[4,256]{1,0:T(4,128)S(1)} %bitcast.17), custom_call_target="tpu_custom_call" | custom-call | tf_op jit(solution)/shard_map/pallas_call | solution.py:247
  70.4 2.0 %copy.7 = f32[256,1,1024]{2,1,0:T(1,128)} copy(f32[256,1,1024]{2,0,1:T(8,128)S(1)} %bitcast.12) | data formatting | bytes 2097152 | tf_op jit(solution)/shard_map/reshape | solution.py:275
  (1 shorter events, 0.0 us)
Async XLA Ops:
  0.0 0.7 copy-start.4
  0.0 1.8 %copy-start.3 = (f32[256,1,1024]{2,1,0:T(1,128)S(1)}, f32[256,1,1024]{2,1,0:T(1,128)}, u32[]{:S(2)}) copy-start(f32[256,1,1024]{2,1,0:T(1,128)} %param.6) | copy-start | bytes 3145732
  1.8 1.0 %copy-start = (bf16[256,1,1024]{2,0,1:T(8,128)(2,1)S(1)}, bf16[256,1,1024]{2,0,1:T(8,128)(2,1)}, u32[]{:S(2)}) copy-start(bf16[256,1,1024]{2,0,1:T(8,128)(2,1)} %param.7) | copy-start | bytes 1572868
  1.8 1.1 %copy-start.1 = (f32[4,1,32,256]{3,2,1,0:T(8,128)S(1)}, f32[4,1,32,256]{3,2,1,0:T(8,128)}, u32[]{:S(2)}) copy-start(f32[4,1,32,256]{3,2,1,0:T(8,128)} %param.9) | copy-start | bytes 393220
  1.8 1.1 %copy-start.2 = (f32[4,1,32,256]{3,2,1,0:T(8,128)S(1)}, f32[4,1,32,256]{3,2,1,0:T(8,128)}, u32[]{:S(2)}) copy-start(f32[4,1,32,256]{3,2,1,0:T(8,128)} %param.10) | copy-start | bytes 393220

commit v2 on v1

--- a/solution.py
+++ b/solution.py
@@ -72,9 +72,16 @@
     def target(row, m, s):
         return (row <= m) & (row + m < d[s])
 
+    def wants_row(col, s):
+        hit = col == r % C
+        for u in range(U):
+            hit = hit | target(r, col + C * u, s)
+        return hit
+
     rows = pl.ds(pl.multiple_of(r * SR, SR), SR)
-    for src, base in ((cofactor, 0), (factor, 2)):
-        for s in range(STEPS):
+
+    def send_operators(s):
+        for src, base in ((cofactor, 0), (factor, 2)):
             for u in range(U):
                 m = c + C * u
                 if u >= U // 2 - s:
@@ -84,15 +91,26 @@
                 if u < U // 2:
                     send_or_local(m < R, src.at[u], ops.at[base, rows],
                                   ops_sem.at[base], (m, owner(m, s)))
-    for s in range(STEPS):
-        send_or_local(c == r % C, rates, ebuf, e_sem.at[0], (r, o[s]))
-
-    def send_lower(s):
+
+    def from_upper(u):
+        return (u + 1) * C <= H
+
+    def send_lower(s, slots):
         to = (r + R - s - H) % R
-        for u in reversed(range(U)):
-            m = c + C * u
-            send(target(to, m, s) & (to + s < R), lower.at[:, slot(u)], atb.at[s, u],
-                 at_sem.at[s, u], (to, c))
+        for u in slots:
+            if not from_upper(u):
+                m = c + C * u
+                send(target(to, m, s) & (to + s < R), lower.at[:, slot(u)], atb.at[s, u],
+                     at_sem.at[s, u], (to, c))
+
+    def send_plain(s):
+        m = r
+        to_u = jnp.minimum(m // C, U - 1)
+        for u in range(H // C + 1):
+            i = c + C * u - s
+            reach = (i >= 0) & (m < (H // C) * C) & target(i, m, s)
+            send_or_local(reach, upper.at[:, slot(u)], atb.at[s, to_u],
+                          at_sem.at[s, to_u], (i, m % C))
 
     def send_upper():
         for u in range(U):
@@ -102,22 +120,36 @@
             send((m >= 0) & target(r, m, 1), upper.at[:, slot(u)], an.at[to_u],
                  an_sem.at[to_u], (r, to))
 
-    send_lower(0)
-    send_upper()
+    for s in range(STEPS):
+        send_or_local(c == r % C, rates, ebuf, e_sem.at[0], (r, o[s]))
+    send_operators(0)
+    send_operators(1)
+    send_lower(0, range(U - 1, U // 2 - 1, -1))
+    send_plain(0)
     out[...] = state[...]
 
-    def spread(s):
+    def spread(s, who=True):
         own_col = r % C == c
         k = jnp.where(own_col, r // C, (d[s] - r) // C)
-        for back in range(1, R):
-            to = jnp.maximum(r - back, 0)
-            send((r >= back) & (own_col | (c == o[s])), xz.at[s, U], xz.at[s, k],
-                 xz_sem.at[s, k], (to, c))
+        has = (own_col | (c == o[s])) & who
+
+        def give(cond, to):
+            send(cond & has, xz.at[s, U], xz.at[s, k], xz_sem.at[s, k], (to, c))
+
+        give(r % 2 == 1, jnp.maximum(r - 1, 0))
+        for back in range(1, R // 2):
+            pair = r // 2 - back
+            give(pair >= 0, jnp.maximum(2 * pair + 1 - r % 2, 0))
 
     def share_row(s):
         for hop in range(1, C):
             to = (c + C - hop) % C
-            send(c == o[s], xz.at[s, U], xz.at[s, U], xz_sem.at[s, U], (r, to))
+            send((c == o[s]) & wants_row(to, s), xz.at[s, U], xz.at[s, U], xz_sem.at[s, U], (r, to))
+
+    def await_row(s):
+        @pl.when(wants_row(c, s))
+        def _():
+            arrive(xz.at[s, U], xz_sem.at[s, U])
 
     def solve(s):
         q = (d[s] - r) // C
@@ -141,45 +173,60 @@
         k = jnp.where(j == r, U, jnp.where(j % C == c, j // C, u))
         return j, k
 
-    def await_z(u, s):
+    def collect(u, s, extra=True):
         j, k = z_index(u, s)
         landed = r < j
         if u >= U // 2:
             landed = landed & (j % C != c)
+        landed = landed & extra
 
         @pl.when(landed)
         def _():
             arrive(xz.at[s, u], xz_sem.at[s, u])
 
-    def update(u, s):
+        send(landed & (r // 2 < j // 2) & (r % 2 != j % 2), xz.at[s, u], xz.at[s, u],
+             xz_sem.at[s, u], (r + 1 - 2 * (r % 2), c))
+
+    def right(u, s):
+        arrive(atb.at[s, u], at_sem.at[s, u])
+        xh, xl = halves(xz[s, U])
+        at = atb[s, u]
+        dims = NT if from_upper(u) else NN
+        out[:, slot(u)] -= mm(xh, at, dims) + mm(xl, at, dims)
+
+    def left(u, s):
         m = c + C * u
         j, k = z_index(u, s)
-        arrive(atb.at[s, u], at_sem.at[s, u])
         if s > 0:
             arrive(an.at[u], an_sem.at[u])
             a = an[u]
         else:
             a = upper[:, slot(u)]
-        xh, xl = halves(xz[s, U])
-        at = atb[s, u]
-        out[:, slot(u)] -= mm(xh, at, NN) + mm(xl, at, NN)
         zh, zl = halves(xz[s, k])
-        straight = d[s] - m <= m
-
-        @pl.when(straight)
-        def _():
-            out[:, slot(u)] -= mm(a, zh, NN) + mm(a, zl, NN)
-
-        @pl.when(jnp.logical_not(straight))
-        def _():
-            out[:, slot(u)] -= mm(a, zh, NT) + mm(a, zl, NT)
-
-    def step_update(u, s):
-        await_z(u, s)
-
-        @pl.when(target(r, c + C * u, s))
-        def _():
-            update(u, s)
+
+        def apply(dims):
+            out[:, slot(u)] -= mm(a, zh, dims) + mm(a, zl, dims)
+
+        low, high = C * u, C * u + C - 1
+        if 2 * low >= d[s]:
+            apply(NN)
+        elif 2 * high < d[s]:
+            apply(NT)
+        else:
+            straight = d[s] - m <= m
+            pl.when(straight)(lambda: apply(NN))
+            pl.when(jnp.logical_not(straight))(lambda: apply(NT))
+
+    def on_targets(s, fns, but=None):
+        for u in range(U):
+            live = target(r, c + C * u, s)
+            if but is not None:
+                live = live & jnp.logical_not(but(u))
+
+            @pl.when(live)
+            def _(u=u):
+                for fn in fns:
+                    fn(u, s)
 
     @pl.when(c == o[0])
     def _():
@@ -187,18 +234,28 @@
 
     @pl.when(c != o[0])
     def _():
-        arrive(xz.at[0, U], xz_sem.at[0, U])
+        await_row(0)
 
     share_row(0)
     spread(0)
-    send_lower(1)
+    send_lower(0, range(U // 2 - 1, -1, -1))
+    send_upper()
+    send_lower(1, range(U - 1, -1, -1))
+    send_plain(1)
 
     q1 = (d[1] - r) // C
     first = c == o[1]
+
+    def picked(u):
+        return first & (q1 == u)
+
     for u in range(U // 2 - 1, U):
-        @pl.when(first & (q1 == u))
+        collect(u, 0, picked(u))
+
+        @pl.when(picked(u))
         def _(u=u):
-            step_update(u, 0)
+            right(u, 0)
+            left(u, 0)
 
     @pl.when(first)
     def _():
@@ -207,26 +264,22 @@
     share_row(1)
 
     def rest():
-        for u in range(U):
-            skip = first & (q1 == u)
-
-            @pl.when(jnp.logical_not(skip))
-            def _(u=u):
-                step_update(u, 0)
+        on_targets(0, (right, left), picked)
+
+    spread(1, first)
+    for u in range(U):
+        collect(u, 0, jnp.logical_not(picked(u)))
+    rest()
 
     @pl.when(jnp.logical_not(first))
     def _():
-        rest()
-        arrive(xz.at[1, U], xz_sem.at[1, U])
-
-    spread(1)
-
-    @pl.when(first)
-    def _():
-        rest()
-
+        await_row(1)
+
+    spread(1, jnp.logical_not(first))
+    on_targets(1, (right,))
     for u in range(U):
-        step_update(u, 1)
+        collect(u, 1)
+    on_targets(1, (left,))
 
     for cond, copy in sends:
         @pl.when(cond)
@@ -242,7 +295,7 @@
     SR = factor.shape[2]
     flat = U * BS
     vmem = pl.BlockSpec(memory_space=pltpu.VMEM)
-    n_sends = 2 * STEPS * (2 * U) + STEPS + (STEPS + 1) * U + STEPS * (R - 1 + C - 1)
+    n_sends = 2 * STEPS * (2 * U) + (STEPS + 8) * (2 * U) + STEPS * (2 * R + C)
     dma = pltpu.SemaphoreType.DMA
     out = pl.pallas_call(
         functools.partial(kernel, R, C, U, BS, SR),

time: 72.6 us -> 70.5 us (0.971)
  Pallas kernels: 67.5 us -> 65.4 us
    pallas_call x1, Pallas kernels: 67.5 us -> 65.4 us  [on_device(): pl.pallas_call(functools.partial(kernel, R, C, U, BS, SR), out_shape=jax....]
where the time goes in v2:
time: 70.5 us; the launch traced here: 70.3 us
  Pallas kernels  65.4 us (93%)
  local copies, waits for them, and re-layouts  4.89 us (7%)
    pallas_call x1, Pallas kernels, on_device(): pl.pallas_call(functools.partial(kernel, R, C, U, BS, SR), out_shape=jax....  65.4 us
    reshape x1, local copies, waits for them, and re-layouts, on_device(): return out.reshape(BS, 1, flat)  2.05 us
    unnamed x12, local copies, waits for them, and re-layouts  1.76 us

profile of v2, /device:TPU:16, one launch (start us, length us, event | category | flops | bytes accessed | tf_op | source)
XLA Modules:
  0.0 70.3 jit_solution(4185988220406676678)
XLA Ops:
  0.0 0.0 copy-start.4
  0.0 0.0 copy-start.3
  0.0 0.7 copy-done.4
  0.7 1.1 %slice_bitcast_fusion.lower = bf16[256,1024]{1,0:T(8,128)(2,1)S(1)} fusion(bf16[2,256,1,1024]{3,1,2,0:T(8,128)(2,1)} %param.8), kind=kLoop, calls=%fused_computation.1 | loop fusion | bytes 1048576 | tf_op jit(solution)/shard_map/reshape;squeeze | solution.py:323
  1.8 0.0 copy-done.3
  1.8 0.0 copy-start
  1.8 0.0 copy-start.1
  1.8 0.0 copy-start.2
  1.8 0.2 copy.12
  2.0 0.8 %copy-done = bf16[256,1,1024]{2,0,1:T(8,128)(2,1)S(1)} copy-done((bf16[256,1,1024]{2,0,1:T(8,128)(2,1)S(1)}, bf16[256,1,1024]{2,0,1:T(8,128)(2,1)}, u32[]{:S(2)}) %copy-start) | copy-done | bytes 524312
  2.8 0.0 copy-done.1
  2.8 0.0 copy-done.2
  2.9 65.4 %shard_map.64 = f32[256,1024]{1,0:T(8,128)S(1)} custom-call(f32[256,1024]{1,0:T(8,128)S(1)} %bitcast.13, bf16[256,1024]{1,0:T(8,128)(2,1)S(1)} %bitcast.14, bf16[256,1024]{1,0:T(8,128)(2,1)S(1)} %slice_bitcast_fusion.lower, f32[4,32,256]{2,1,0:T(8,128)S(1)} %bitcast.15, f32[4,32,256]{2,1,0:T(8,128)S(1)} %bitcast.16, f32[4,256]{1,0:T(4,128)S(1)} %bitcast.17), custom_call_target="tpu_custom_call" | custom-call | tf_op jit(solution)/shard_map/pallas_call | solution.py:300
  68.3 2.0 %copy.7 = f32[256,1,1024]{2,1,0:T(1,128)} copy(f32[256,1,1024]{2,0,1:T(8,128)S(1)} %bitcast.12) | data formatting | bytes 2097152 | tf_op jit(solution)/shard_map/reshape | solution.py:328
  (1 shorter events, 0.0 us)
Async XLA Ops:
  0.0 0.7 copy-start.4
  0.0 1.8 %copy-start.3 = (f32[256,1,1024]{2,1,0:T(1,128)S(1)}, f32[256,1,1024]{2,1,0:T(1,128)}, u32[]{:S(2)}) copy-start(f32[256,1,1024]{2,1,0:T(1,128)} %param.6) | copy-start | bytes 3145732
  1.8 1.0 %copy-start = (bf16[256,1,1024]{2,0,1:T(8,128)(2,1)S(1)}, bf16[256,1,1024]{2,0,1:T(8,128)(2,1)}, u32[]{:S(2)}) copy-start(bf16[256,1,1024]{2,0,1:T(8,128)(2,1)} %param.7) | copy-start | bytes 1572868
  1.8 1.1 %copy-start.1 = (f32[4,1,32,256]{3,2,1,0:T(8,128)S(1)}, f32[4,1,32,256]{3,2,1,0:T(8,128)}, u32[]{:S(2)}) copy-start(f32[4,1,32,256]{3,2,1,0:T(8,128)} %param.9) | copy-start | bytes 393220
  1.8 1.1 %copy-start.2 = (f32[4,1,32,256]{3,2,1,0:T(8,128)S(1)}, f32[4,1,32,256]{3,2,1,0:T(8,128)}, u32[]{:S(2)}) copy-start(f32[4,1,32,256]{3,2,1,0:T(8,128)} %param.10) | copy-start | bytes 393220

commit v3 on v2

--- a/solution.py
+++ b/solution.py
@@ -71,12 +71,6 @@
 
     def target(row, m, s):
         return (row <= m) & (row + m < d[s])
-
-    def wants_row(col, s):
-        hit = col == r % C
-        for u in range(U):
-            hit = hit | target(r, col + C * u, s)
-        return hit
 
     rows = pl.ds(pl.multiple_of(r * SR, SR), SR)
 
@@ -124,6 +118,7 @@
         send_or_local(c == r % C, rates, ebuf, e_sem.at[0], (r, o[s]))
     send_operators(0)
     send_operators(1)
+    send_upper()
     send_lower(0, range(U - 1, U // 2 - 1, -1))
     send_plain(0)
     out[...] = state[...]
@@ -141,15 +136,32 @@
             pair = r // 2 - back
             give(pair >= 0, jnp.maximum(2 * pair + 1 - r % 2, 0))
 
-    def share_row(s):
-        for hop in range(1, C):
-            to = (c + C - hop) % C
-            send((c == o[s]) & wants_row(to, s), xz.at[s, U], xz.at[s, U], xz_sem.at[s, U], (r, to))
-
-    def await_row(s):
-        @pl.when(wants_row(c, s))
-        def _():
-            arrive(xz.at[s, U], xz_sem.at[s, U])
+    def half(h):
+        return pl.ds(h * (BS // 2), BS // 2)
+
+    def pass_row(s, h, who=True):
+        block = xz.at[s, U, half(h)]
+        sem = xz_sem.at[s, U + h]
+        far = o[s] == 0
+        up = (c >= o[s]) & (c < C - 1)
+        if s == 0:
+            send((c == o[s]) & far & who, block, block, sem, (r, C - 1))
+            up = up & jnp.logical_not(far & (c == C - 2))
+        send((c <= o[s]) & (c >= 1) & who, block, block, sem, (r, jnp.maximum(c - 1, 0)))
+        send(up & who, block, block, sem, (r, jnp.minimum(c + 1, C - 1)))
+
+    def take_row(s):
+        other = c != o[s]
+        for h in range(2):
+            @pl.when(other)
+            def _(h=h):
+                arrive(xz.at[s, U, half(h)], xz_sem.at[s, U + h])
+
+            pass_row(s, h, other)
+
+    def give_row(s):
+        for h in range(2):
+            pass_row(s, h, c == o[s])
 
     def solve(s):
         q = (d[s] - r) // C
@@ -232,14 +244,10 @@
     def _():
         solve(0)
 
-    @pl.when(c != o[0])
-    def _():
-        await_row(0)
-
-    share_row(0)
+    give_row(0)
+    take_row(0)
     spread(0)
     send_lower(0, range(U // 2 - 1, -1, -1))
-    send_upper()
     send_lower(1, range(U - 1, -1, -1))
     send_plain(1)
 
@@ -261,7 +269,7 @@
     def _():
         solve(1)
 
-    share_row(1)
+    give_row(1)
 
     def rest():
         on_targets(0, (right, left), picked)
@@ -271,10 +279,7 @@
         collect(u, 0, jnp.logical_not(picked(u)))
     rest()
 
-    @pl.when(jnp.logical_not(first))
-    def _():
-        await_row(1)
-
+    take_row(1)
     spread(1, jnp.logical_not(first))
     on_targets(1, (right,))
     for u in range(U):
@@ -295,7 +300,7 @@
     SR = factor.shape[2]
     flat = U * BS
     vmem = pl.BlockSpec(memory_space=pltpu.VMEM)
-    n_sends = 2 * STEPS * (2 * U) + (STEPS + 8) * (2 * U) + STEPS * (2 * R + C)
+    n_sends = 2 * STEPS * (2 * U) + (STEPS + 8) * (2 * U) + STEPS * (2 * R + 16)
     dma = pltpu.SemaphoreType.DMA
     out = pl.pallas_call(
         functools.partial(kernel, R, C, U, BS, SR),
@@ -310,7 +315,7 @@
             pltpu.VMEM((U, BS, BS), jnp.bfloat16),
             dma((4,)),
             dma((1,)),
-            dma((STEPS, U + 1)),
+            dma((STEPS, U + 2)),
             dma((STEPS, U)),
             dma((U,)),
             dma((n_sends,)),

time: 70.5 us -> 63.6 us (0.902)
  Pallas kernels: 65.4 us -> 58.5 us
    pallas_call x1, Pallas kernels: 65.4 us -> 58.5 us  [on_device(): pl.pallas_call(functools.partial(kernel, R, C, U, BS, SR), out_shape=jax....]
where the time goes in v3:
time: 63.6 us; the launch traced here: 63.4 us
  Pallas kernels  58.5 us (92%)
  local copies, waits for them, and re-layouts  4.89 us (8%)
    pallas_call x1, Pallas kernels, on_device(): pl.pallas_call(functools.partial(kernel, R, C, U, BS, SR), out_shape=jax....  58.5 us
    reshape x1, local copies, waits for them, and re-layouts, on_device(): return out.reshape(BS, 1, flat)  2.05 us
    unnamed x12, local copies, waits for them, and re-layouts  1.76 us

profile of v3, /device:TPU:16, one launch (start us, length us, event | category | flops | bytes accessed | tf_op | source)
XLA Modules:
  0.0 63.4 jit_solution(9851298328847732363)
XLA Ops:
  0.0 0.0 copy-start.4
  0.0 0.0 copy-start.3
  0.0 0.7 %copy-done.4 = f32[4,1,256]{2,1,0:T(1,128)S(1)} copy-done((f32[4,1,256]{2,1,0:T(1,128)S(1)}, f32[4,1,256]{2,1,0:T(1,128)}, u32[]{:S(2)}) %copy-start.4) | copy-done | bytes 4120
  0.7 1.1 %slice_bitcast_fusion.lower = bf16[256,1024]{1,0:T(8,128)(2,1)S(1)} fusion(bf16[2,256,1,1024]{3,1,2,0:T(8,128)(2,1)} %param.8), kind=kLoop, calls=%fused_computation.1 | loop fusion | bytes 1048576 | tf_op jit(solution)/shard_map/reshape;squeeze | solution.py:328
  1.8 0.0 copy-done.3
  1.8 0.0 copy-start
  1.8 0.0 copy-start.1
  1.8 0.0 copy-start.2
  1.8 0.2 copy.12
  2.0 0.8 %copy-done = bf16[256,1,1024]{2,0,1:T(8,128)(2,1)S(1)} copy-done((bf16[256,1,1024]{2,0,1:T(8,128)(2,1)S(1)}, bf16[256,1,1024]{2,0,1:T(8,128)(2,1)}, u32[]{:S(2)}) %copy-start) | copy-done | bytes 524312
  2.8 0.0 copy-done.1
  2.8 0.0 copy-done.2
  2.9 58.5 %shard_map.64 = f32[256,1024]{1,0:T(8,128)S(1)} custom-call(f32[256,1024]{1,0:T(8,128)S(1)} %bitcast.13, bf16[256,1024]{1,0:T(8,128)(2,1)S(1)} %bitcast.14, bf16[256,1024]{1,0:T(8,128)(2,1)S(1)} %slice_bitcast_fusion.lower, f32[4,32,256]{2,1,0:T(8,128)S(1)} %bitcast.15, f32[4,32,256]{2,1,0:T(8,128)S(1)} %bitcast.16, f32[4,256]{1,0:T(4,128)S(1)} %bitcast.17), custom_call_target="tpu_custom_call" | custom-call | tf_op jit(solution)/shard_map/pallas_call | solution.py:305
  61.4 2.0 %copy.7 = f32[256,1,1024]{2,1,0:T(1,128)} copy(f32[256,1,1024]{2,0,1:T(8,128)S(1)} %bitcast.12) | data formatting | bytes 2097152 | tf_op jit(solution)/shard_map/reshape | solution.py:333
  (1 shorter events, 0.0 us)
Async XLA Ops:
  0.0 0.7 %copy-start.4 = (f32[4,1,256]{2,1,0:T(1,128)S(1)}, f32[4,1,256]{2,1,0:T(1,128)}, u32[]{:S(2)}) copy-start(f32[4,1,256]{2,1,0:T(1,128)} %param.11) | copy-start | bytes 12292
  0.0 1.8 %copy-start.3 = (f32[256,1,1024]{2,1,0:T(1,128)S(1)}, f32[256,1,1024]{2,1,0:T(1,128)}, u32[]{:S(2)}) copy-start(f32[256,1,1024]{2,1,0:T(1,128)} %param.6) | copy-start | bytes 3145732
  1.8 1.0 %copy-start = (bf16[256,1,1024]{2,0,1:T(8,128)(2,1)S(1)}, bf16[256,1,1024]{2,0,1:T(8,128)(2,1)}, u32[]{:S(2)}) copy-start(bf16[256,1,1024]{2,0,1:T(8,128)(2,1)} %param.7) | copy-start | bytes 1572868
  1.8 1.1 %copy-start.1 = (f32[4,1,32,256]{3,2,1,0:T(8,128)S(1)}, f32[4,1,32,256]{3,2,1,0:T(8,128)}, u32[]{:S(2)}) copy-start(f32[4,1,32,256]{3,2,1,0:T(8,128)} %param.9) | copy-start | bytes 393220
  1.8 1.1 %copy-start.2 = (f32[4,1,32,256]{3,2,1,0:T(8,128)S(1)}, f32[4,1,32,256]{3,2,1,0:T(8,128)}, u32[]{:S(2)}) copy-start(f32[4,1,32,256]{3,2,1,0:T(8,128)} %param.10) | copy-start | bytes 393220

commit v4 on v3

--- a/solution.py
+++ b/solution.py
@@ -8,6 +8,7 @@
 from jax.sharding import PartitionSpec as P
 
 STEPS = 2
+CHUNKS = 4
 MESH = pl.DeviceIdType.MESH
 F32 = jnp.float32
 NN = (((1,), (0,)), ((), ()))
@@ -41,6 +42,16 @@
 
     o = [owner(r, s) for s in range(STEPS)]
     sends = []
+    me = r * C + c
+
+    barrier = pltpu.get_barrier_semaphore()
+
+    @pl.loop(1, R * C)
+    def _(k):
+        peer = (me + k) % (R * C)
+        pl.semaphore_signal(barrier, inc=1, device_id=(peer // C, peer % C), device_id_type=MESH)
+
+    pl.semaphore_wait(barrier, R * C - 1)
 
     def send(cond, src, dst, sem, dev):
         k = len(sends)
@@ -123,25 +134,25 @@
     send_plain(0)
     out[...] = state[...]
 
-    def spread(s, who=True):
+    def spread(s, h, who):
         own_col = r % C == c
         k = jnp.where(own_col, r // C, (d[s] - r) // C)
         has = (own_col | (c == o[s])) & who
 
         def give(cond, to):
-            send(cond & has, xz.at[s, U], xz.at[s, k], xz_sem.at[s, k], (to, c))
+            send(cond & has, xz.at[s, U, part(h)], xz.at[s, k, part(h)], xz_sem.at[s, k, h], (to, c))
 
         give(r % 2 == 1, jnp.maximum(r - 1, 0))
         for back in range(1, R // 2):
             pair = r // 2 - back
             give(pair >= 0, jnp.maximum(2 * pair + 1 - r % 2, 0))
 
-    def half(h):
-        return pl.ds(h * (BS // 2), BS // 2)
+    def part(h):
+        return pl.ds(h * (BS // CHUNKS), BS // CHUNKS)
 
     def pass_row(s, h, who=True):
-        block = xz.at[s, U, half(h)]
-        sem = xz_sem.at[s, U + h]
+        block = xz.at[s, U, part(h)]
+        sem = xz_sem.at[s, U, h]
         far = o[s] == 0
         up = (c >= o[s]) & (c < C - 1)
         if s == 0:
@@ -152,16 +163,18 @@
 
     def take_row(s):
         other = c != o[s]
-        for h in range(2):
+        for h in range(CHUNKS):
             @pl.when(other)
             def _(h=h):
-                arrive(xz.at[s, U, half(h)], xz_sem.at[s, U + h])
+                arrive(xz.at[s, U, part(h)], xz_sem.at[s, U, h])
 
             pass_row(s, h, other)
+            spread(s, h, other)
 
     def give_row(s):
-        for h in range(2):
+        for h in range(CHUNKS):
             pass_row(s, h, c == o[s])
+            spread(s, h, c == o[s])
 
     def solve(s):
         q = (d[s] - r) // C
@@ -192,12 +205,15 @@
             landed = landed & (j % C != c)
         landed = landed & extra
 
-        @pl.when(landed)
-        def _():
-            arrive(xz.at[s, u], xz_sem.at[s, u])
-
-        send(landed & (r // 2 < j // 2) & (r % 2 != j % 2), xz.at[s, u], xz.at[s, u],
-             xz_sem.at[s, u], (r + 1 - 2 * (r % 2), c))
+        for h in range(CHUNKS):
+            block = xz.at[s, u, part(h)]
+
+            @pl.when(landed)
+            def _(block=block, h=h):
+                arrive(block, xz_sem.at[s, u, h])
+
+            send(landed & (r // 2 < j // 2) & (r % 2 != j % 2), block, block,
+                 xz_sem.at[s, u, h], (r + 1 - 2 * (r % 2), c))
 
     def right(u, s):
         arrive(atb.at[s, u], at_sem.at[s, u])
@@ -246,7 +262,6 @@
 
     give_row(0)
     take_row(0)
-    spread(0)
     send_lower(0, range(U // 2 - 1, -1, -1))
     send_lower(1, range(U - 1, -1, -1))
     send_plain(1)
@@ -274,13 +289,11 @@
     def rest():
         on_targets(0, (right, left), picked)
 
-    spread(1, first)
     for u in range(U):
         collect(u, 0, jnp.logical_not(picked(u)))
     rest()
 
     take_row(1)
-    spread(1, jnp.logical_not(first))
     on_targets(1, (right,))
     for u in range(U):
         collect(u, 1)
@@ -300,7 +313,7 @@
     SR = factor.shape[2]
     flat = U * BS
     vmem = pl.BlockSpec(memory_space=pltpu.VMEM)
-    n_sends = 2 * STEPS * (2 * U) + (STEPS + 8) * (2 * U) + STEPS * (2 * R + 16)
+    n_sends = 2 * STEPS * (2 * U) + (STEPS + 8) * (2 * U) + STEPS * CHUNKS * (R + 2 * U + 8)
     dma = pltpu.SemaphoreType.DMA
     out = pl.pallas_call(
         functools.partial(kernel, R, C, U, BS, SR),
@@ -315,13 +328,13 @@
             pltpu.VMEM((U, BS, BS), jnp.bfloat16),
             dma((4,)),
             dma((1,)),
-            dma((STEPS, U + 2)),
+            dma((STEPS, U + 1, CHUNKS)),
             dma((STEPS, U)),
             dma((U,)),
             dma((n_sends,)),
         ],
         compiler_params=pltpu.CompilerParams(
-            has_side_effects=True, vmem_limit_bytes=48 * 1024 * 1024),
+            collective_id=0, has_side_effects=True, vmem_limit_bytes=48 * 1024 * 1024),
     )(
         state.reshape(BS, flat),
         coupling.reshape(BS, flat),

time: 63.6 us -> 60.7 us (0.954)
  Pallas kernels: 58.5 us -> 55.6 us
    pallas_call x1, Pallas kernels: 58.5 us -> 55.6 us  [on_device(): pl.pallas_call(functools.partial(kernel, R, C, U, BS, SR), out_shape=jax....]
where the time goes in v4:
time: 60.7 us; the launch traced here: 60.5 us
  Pallas kernels  55.6 us (92%)
  local copies, waits for them, and re-layouts  4.89 us (8%)
    pallas_call x1, Pallas kernels, on_device(): pl.pallas_call(functools.partial(kernel, R, C, U, BS, SR), out_shape=jax....  55.6 us
    reshape x1, local copies, waits for them, and re-layouts, on_device(): return out.reshape(BS, 1, flat)  2.05 us
    unnamed x12, local copies, waits for them, and re-layouts  1.76 us

profile of v4, /device:TPU:16, one launch (start us, length us, event | category | flops | bytes accessed | tf_op | source)
XLA Modules:
  0.0 60.5 jit_solution(8700275264411596352)
XLA Ops:
  0.0 0.0 copy-start.4
  0.0 0.0 copy-start.3
  0.0 0.7 %copy-done.4 = f32[4,1,256]{2,1,0:T(1,128)S(1)} copy-done((f32[4,1,256]{2,1,0:T(1,128)S(1)}, f32[4,1,256]{2,1,0:T(1,128)}, u32[]{:S(2)}) %copy-start.4) | copy-done | bytes 4120
  0.7 1.1 %slice_bitcast_fusion.lower = bf16[256,1024]{1,0:T(8,128)(2,1)S(1)} fusion(bf16[2,256,1,1024]{3,1,2,0:T(8,128)(2,1)} %param.8), kind=kLoop, calls=%fused_computation.1 | loop fusion | bytes 1048576 | tf_op jit(solution)/shard_map/reshape;squeeze | solution.py:341
  1.8 0.0 copy-done.3
  1.8 0.0 copy-start
  1.8 0.0 copy-start.1
  1.8 0.0 copy-start.2
  1.8 0.2 copy.12
  2.0 0.8 %copy-done = bf16[256,1,1024]{2,0,1:T(8,128)(2,1)S(1)} copy-done((bf16[256,1,1024]{2,0,1:T(8,128)(2,1)S(1)}, bf16[256,1,1024]{2,0,1:T(8,128)(2,1)}, u32[]{:S(2)}) %copy-start) | copy-done | bytes 524312
  2.8 0.0 copy-done.1
  2.8 0.0 copy-done.2
  2.9 55.6 %shard_map.64 = f32[256,1024]{1,0:T(8,128)S(1)} custom-call(f32[256,1024]{1,0:T(8,128)S(1)} %bitcast.13, bf16[256,1024]{1,0:T(8,128)(2,1)S(1)} %bitcast.14, bf16[256,1024]{1,0:T(8,128)(2,1)S(1)} %slice_bitcast_fusion.lower, f32[4,32,256]{2,1,0:T(8,128)S(1)} %bitcast.15, f32[4,32,256]{2,1,0:T(8,128)S(1)} %bitcast.16, f32[4,256]{1,0:T(4,128)S(1)} %bitcast.17), custom_call_target="tpu_custom_call" | custom-call | tf_op jit(solution)/shard_map/pallas_call | solution.py:318
  58.5 2.0 %copy.7 = f32[256,1,1024]{2,1,0:T(1,128)} copy(f32[256,1,1024]{2,0,1:T(8,128)S(1)} %bitcast.12) | data formatting | bytes 2097152 | tf_op jit(solution)/shard_map/reshape | solution.py:346
  (1 shorter events, 0.0 us)
Async XLA Ops:
  0.0 0.7 %copy-start.4 = (f32[4,1,256]{2,1,0:T(1,128)S(1)}, f32[4,1,256]{2,1,0:T(1,128)}, u32[]{:S(2)}) copy-start(f32[4,1,256]{2,1,0:T(1,128)} %param.11) | copy-start | bytes 12292
  0.0 1.8 %copy-start.3 = (f32[256,1,1024]{2,1,0:T(1,128)S(1)}, f32[256,1,1024]{2,1,0:T(1,128)}, u32[]{:S(2)}) copy-start(f32[256,1,1024]{2,1,0:T(1,128)} %param.6) | copy-start | bytes 3145732
  1.8 1.0 %copy-start = (bf16[256,1,1024]{2,0,1:T(8,128)(2,1)S(1)}, bf16[256,1,1024]{2,0,1:T(8,128)(2,1)}, u32[]{:S(2)}) copy-start(bf16[256,1,1024]{2,0,1:T(8,128)(2,1)} %param.7) | copy-start | bytes 1572868
  1.8 1.1 %copy-start.1 = (f32[4,1,32,256]{3,2,1,0:T(8,128)S(1)}, f32[4,1,32,256]{3,2,1,0:T(8,128)}, u32[]{:S(2)}) copy-start(f32[4,1,32,256]{3,2,1,0:T(8,128)} %param.9) | copy-start | bytes 393220
  1.8 1.1 %copy-start.2 = (f32[4,1,32,256]{3,2,1,0:T(8,128)S(1)}, f32[4,1,32,256]{3,2,1,0:T(8,128)}, u32[]{:S(2)}) copy-start(f32[4,1,32,256]{3,2,1,0:T(8,128)} %param.10) | copy-start | bytes 393220

commit v5 on v4

--- a/solution.py
+++ b/solution.py
@@ -105,7 +105,7 @@
         for u in slots:
             if not from_upper(u):
                 m = c + C * u
-                send(target(to, m, s) & (to + s < R), lower.at[:, slot(u)], atb.at[s, u],
+                send(target(to, m, s) & (to + s < R), lower.at[0, :, slot(u)], atb.at[s, u],
                      at_sem.at[s, u], (to, c))
 
     def send_plain(s):
@@ -313,12 +313,13 @@
     SR = factor.shape[2]
     flat = U * BS
     vmem = pl.BlockSpec(memory_space=pltpu.VMEM)
+    hbm = pl.BlockSpec(memory_space=pl.ANY)
     n_sends = 2 * STEPS * (2 * U) + (STEPS + 8) * (2 * U) + STEPS * CHUNKS * (R + 2 * U + 8)
     dma = pltpu.SemaphoreType.DMA
     out = pl.pallas_call(
         functools.partial(kernel, R, C, U, BS, SR),
         out_shape=jax.ShapeDtypeStruct((BS, flat), F32),
-        in_specs=[vmem] * 6,
+        in_specs=[vmem, vmem, hbm, vmem, vmem, vmem],
         out_specs=vmem,
         scratch_shapes=[
             pltpu.VMEM((4, BS, BS), F32),
@@ -338,7 +339,7 @@
     )(
         state.reshape(BS, flat),
         coupling.reshape(BS, flat),
-        coupling_t[0].reshape(BS, flat),
+        coupling_t.reshape(coupling_t.shape[0], BS, flat),
         factor.reshape(U, SR, BS),
         cofactor.reshape(U, SR, BS),
         rates.reshape(U, BS),

time: 60.7 us -> 60.3 us (level)
    another operation x1 -> x0, local copies, waits for them, and re-layouts: 1.08 us -> none  [on_device(): coupling_t[0].reshape(BS, flat)]
    unnamed x12, local copies, waits for them, and re-layouts: 1.76 us -> 2.4 us
where the time goes in v5:
time: 60.3 us; the launch traced here: 60.2 us
  Pallas kernels  55.7 us (92%)
  local copies, waits for them, and re-layouts  4.44 us (7%)
    pallas_call x1, Pallas kernels, on_device(): pl.pallas_call(functools.partial(kernel, R, C, U, BS, SR), out_shape=jax....  55.7 us
    unnamed x12, local copies, waits for them, and re-layouts  2.4 us
    reshape x1, local copies, waits for them, and re-layouts, on_device(): return out.reshape(BS, 1, flat)  2.05 us

profile of v5, /device:TPU:16, one launch (start us, length us, event | category | flops | bytes accessed | tf_op | source)
XLA Modules:
  0.0 60.2 jit_solution(8813636587969967112)
XLA Ops:
  0.0 0.0 copy-start.4
  0.0 0.7 %copy-done.4 = f32[4,1,256]{2,1,0:T(1,128)S(1)} copy-done((f32[4,1,256]{2,1,0:T(1,128)S(1)}, f32[4,1,256]{2,1,0:T(1,128)}, u32[]{:S(2)}) %copy-start.4) | copy-done | bytes 4120
  0.7 0.0 copy-start
  0.7 0.0 copy-start.1
  0.7 0.0 copy-start.2
  0.7 0.0 copy-start.3
  0.7 1.6 %copy.12 = f32[256,1,1024]{2,0,1:T(8,128)S(1)} copy(f32[256,1,1024]{2,1,0:T(1,128)} %param.6) | data formatting | bytes 2097152
  2.3 0.0 copy-done
  2.3 0.1 copy-done.1
  2.4 0.0 copy-done.2
  2.4 0.0 copy-done.3
  2.4 55.7 %shard_map.64 = f32[256,1024]{1,0:T(8,128)S(1)} custom-call(f32[256,1024]{1,0:T(8,128)S(1)} %bitcast.12, bf16[256,1024]{1,0:T(8,128)(2,1)S(1)} %bitcast.14, bf16[2,256,1024]{2,1,0:T(8,128)(2,1)S(1)} %bitcast.13, f32[4,32,256]{2,1,0:T(8,128)S(1)} %bitcast.15, f32[4,32,256]{2,1,0:T(8,128)S(1)} %bitcast.16, f32[4,256]{1,0:T(4,128)S(1)} %bitcast.17), custom_call_target="tpu_custom_call" | custom-call | tf_op jit(solution)/shard_map/pallas_call | solution.py:319
  58.1 2.0 %copy.7 = f32[256,1,1024]{2,1,0:T(1,128)} copy(f32[256,1,1024]{2,0,1:T(8,128)S(1)} %bitcast.11) | data formatting | bytes 2097152 | tf_op jit(solution)/shard_map/reshape | solution.py:347
  (1 shorter events, 0.0 us)
Async XLA Ops:
  0.0 0.7 %copy-start.4 = (f32[4,1,256]{2,1,0:T(1,128)S(1)}, f32[4,1,256]{2,1,0:T(1,128)}, u32[]{:S(2)}) copy-start(f32[4,1,256]{2,1,0:T(1,128)} %param.11) | copy-start | bytes 12292
  0.7 1.6 %copy-start = (bf16[2,256,1,1024]{3,1,2,0:T(8,128)(2,1)S(1)}, bf16[2,256,1,1024]{3,1,2,0:T(8,128)(2,1)}, u32[]{:S(2)}) copy-start(bf16[2,256,1,1024]{3,1,2,0:T(8,128)(2,1)} %param.8) | copy-start | bytes 3145732
  0.7 1.7 %copy-start.1 = (bf16[256,1,1024]{2,0,1:T(8,128)(2,1)S(1)}, bf16[256,1,1024]{2,0,1:T(8,128)(2,1)}, u32[]{:S(2)}) copy-start(bf16[256,1,1024]{2,0,1:T(8,128)(2,1)} %param.7) | copy-start | bytes 1572868
  0.7 1.7 %copy-start.2 = (f32[4,1,32,256]{3,2,1,0:T(8,128)S(1)}, f32[4,1,32,256]{3,2,1,0:T(8,128)}, u32[]{:S(2)}) copy-start(f32[4,1,32,256]{3,2,1,0:T(8,128)} %param.9) | copy-start | bytes 393220
  0.7 1.7 %copy-start.3 = (f32[4,1,32,256]{3,2,1,0:T(8,128)S(1)}, f32[4,1,32,256]{3,2,1,0:T(8,128)}, u32[]{:S(2)}) copy-start(f32[4,1,32,256]{3,2,1,0:T(8,128)} %param.10) | copy-start | bytes 393220
